TPU v7x, 32 devices: a whole 2x2x4 slice. The times are simulated.
32 devices in a mesh: epoch: 4 (over y, x), blend: 8 (over z, core).
Axes of the slice: x: 2, y: 2, z: 4, core: 2. Of those that a mesh axis runs over, the one named last changes fastest.
Arguments:
- visit_flux: bfloat16 [16, 32, 6, 16384], P('epoch', None, None, 'blend'), may hold values from -6 to 6
- visit_precision: bfloat16 [16, 32, 6, 16384], P('epoch', None, None, 'blend'), may hold values from 0.25 to 4
- visit_live: int32 [16, 32], P('epoch'), may hold values 0 or 1
- footprint: int32 [32, 8, 16384], P('blend', None, 'epoch'), may hold values 0 or 1
- source_count: int32 [32], P('blend'), may hold values from 1 to 8
- spectra_init: float32 [32, 8, 6], P('blend'), may hold values from 0.2 to 1.2
- morphology_init: float32 [32, 8, 16384], P('blend', None, 'epoch'), may hold values from 0 to 0.25
Outputs:
- coadd_flux: float32 [32, 6, 16384], P('blend', None, 'epoch')
- spectra: float32 [32, 8, 6], P('blend')
- morphology: float32 [32, 8, 16384], P('blend', None, 'epoch')
All inputs are finite; a program needn't handle non-finite values. No bound on the sum of `visit_live` or of `footprint` on one device may be relied on, other than what follows from the above.
Results may differ from a plain program's by a relative error of at most 0.0003.
Values sent between devices are 32-bit elements; how exact they have to be, the bound alone decides.
A program may use at most 64 MiB of HBM per device.

v0:
```python
import jax
import jax.numpy as jnp
from jax import lax
from jax.sharding import PartitionSpec as P

ITERS = 2


def on_device(
    visit_flux, visit_precision, visit_live, footprint, source_count, spectra_init, morphology_init
):
    weights = visit_precision.astype(jnp.float32) * visit_live.astype(jnp.float32)[:, :, None, None]
    numerator = jnp.sum(weights * visit_flux.astype(jnp.float32), axis=0)
    weight_sum = jnp.sum(weights, axis=0)
    pix_part = morphology_init.shape[2]
    owned = morphology_init.shape[0]
    numerator, weight_sum = (
        lax.psum_scatter(numerator, "epoch", scatter_dimension=2, tiled=True),
        lax.psum_scatter(weight_sum, "epoch", scatter_dimension=2, tiled=True),
    )
    every_blend, band_count, piece = numerator.shape
    numerator = numerator.reshape(every_blend, band_count, 1, piece)
    weight_sum = weight_sum.reshape(every_blend, band_count, 1, piece)
    numerator, weight_sum = (
        lax.all_to_all(numerator, "blend", split_axis=0, concat_axis=2, tiled=True),
        lax.all_to_all(weight_sum, "blend", split_axis=0, concat_axis=2, tiled=True),
    )
    blocks = numerator.shape[2]
    numerator = numerator.reshape(owned, band_count, blocks, 1, piece)
    weight_sum = weight_sum.reshape(owned, band_count, blocks, 1, piece)
    numerator, weight_sum = (
        lax.all_to_all(numerator, "epoch", split_axis=2, concat_axis=3, tiled=True),
        lax.all_to_all(weight_sum, "epoch", split_axis=2, concat_axis=3, tiled=True),
    )
    numerator = numerator.reshape(owned, band_count, pix_part)
    weight_sum = weight_sum.reshape(owned, band_count, pix_part)
    coadd_flux = numerator / (1.0 + weight_sum)
    coverage = weight_sum / (1.0 + weight_sum)
    slots = footprint.shape[1]
    source_live = (jnp.arange(slots, dtype=jnp.int32)[None, :] < source_count[:, None]).astype(
        jnp.float32
    )
    footprint_mask = footprint.astype(jnp.float32) * source_live[:, :, None]
    live_count = source_count.astype(jnp.float32)
    morphology = morphology_init * footprint_mask
    spectra = spectra_init
    highest = lax.Precision.HIGHEST
    for iteration in range(ITERS):
        blend_model = jnp.einsum("bkc,bkp->bcp", spectra, morphology, precision=highest)
        residual = coverage * (coadd_flux - blend_model)
        morph_grad = jnp.einsum("bkc,bcp->bkp", spectra, residual, precision=highest)
        morph_step = 1.0 / (1.0 + live_count[:, None] * jnp.sum(spectra * spectra, axis=2))
        morphology = (
            jnp.maximum(0.0, morphology + morph_grad * morph_step[:, :, None]) * footprint_mask
        )
        blend_model = jnp.einsum("bkc,bkp->bcp", spectra, morphology, precision=highest)
        residual = coverage * (coadd_flux - blend_model)
        spectra_grad = jnp.einsum("bkp,bcp->bkc", morphology, residual, precision=highest)
        morph_norm = jnp.sum(morphology * morphology, axis=2)
        spectra_grad, morph_norm = lax.psum((spectra_grad, morph_norm), "epoch")
        spectra = jnp.maximum(
            0.0, spectra + spectra_grad / (1.0 + live_count[:, None] * morph_norm)[:, :, None]
        )
    return (coadd_flux, spectra, morphology)


def solution(mesh):
    in_specs = (
        P("epoch", None, None, "blend"),
        P("epoch", None, None, "blend"),
        P("epoch", None),
        P("blend", None, "epoch"),
        P("blend"),
        P("blend", None, None),
        P("blend", None, "epoch"),
    )
    out_specs = (P("blend", None, "epoch"), P("blend", None, None), P("blend", None, "epoch"))
    return jax.shard_map(
        on_device, mesh=mesh, in_specs=in_specs, out_specs=out_specs, check_vma=False
    )
```

profile of v0, /device:TPU:0, one launch (start us, length us, event | category | flops | bytes accessed | tf_op | source)
XLA Modules:
  0.0 167.4 jit_solution(2619093483653560001)
XLA Ops:
  7.2 0.7 convert_element_type.23
  7.9 6.4 %fusion = (f32[32,6,2048]{2,0,1:T(8,128)}, f32[32,6,2048]{2,0,1:T(8,128)}) fusion(bf16[4,32,6,2048]{3,1,2,0:T(8,128)(2,1)} %param.8, f32[4,32]{1,0:T(4,128)S(1)} %convert_element_type.23, bf16[4,32,6,2048]{3,1,2,0:T(8,128)(2,1)} %param.7), kind=kLoop, calls=%fused_computation.2 | loop fusion | flops 8650752 | bytes 9437696 | tf_op jit(solution)/shard_map/reduce_sum | solution.py:14
  14.4 0.7 reduce-scatter.3.cloned.1.call-update
  15.1 33.3 %reduce-scatter.5.cloned.1.call-done = f32[32,6,512]{2,0,1:T(8,128)} async-done(((f32[32,6,2048]{2,0,1:T(8,128)}), f32[32,6,512]{2,0,1:T(8,128)}) %reduce-scatter.5.cloned.1.call-update) | async-done | bytes 393232 | tf_op jit(solution)/shard_map/reduce_scatter | solution.py:19
  48.4 2.1 %copy.58 = f32[32,6,1,512]{3,2,1,0:T(1,128)} copy(f32[32,6,1,512]{3,0,1,2:T(8,128)} %bitcast.57) | data formatting | bytes 786432 | tf_op jit(solution)/shard_map/reshape | solution.py:23
  50.5 4.6 %all-to-all-start.2 = ((f32[32,6,1,512]{3,2,1,0:T(1,128)}), f32[32,6,1,512]{3,2,1,0:T(1,128)S(1)}, u32[]{:S(2)}, u32[]{:S(2)}) async-start(f32[32,6,1,512]{3,2,1,0:T(1,128)} %copy.58), calls=%async_computation.4 | async-start | bytes 786432 | tf_op jit(solution)/shard_map/all_to_all | solution.py:26
  55.1 27.4 %reduce-scatter.3.cloned.1.call-done = f32[32,6,512]{2,0,1:T(8,128)} async-done(((f32[32,6,2048]{2,0,1:T(8,128)}), f32[32,6,512]{2,0,1:T(8,128)}) %reduce-scatter.3.cloned.1.call-update) | async-done | bytes 393232 | tf_op jit(solution)/shard_map/reduce_scatter | solution.py:18
  82.5 2.1 %copy.54 = f32[32,6,1,512]{3,2,1,0:T(1,128)} copy(f32[32,6,1,512]{3,0,1,2:T(8,128)} %bitcast.58) | data formatting | bytes 786432 | tf_op jit(solution)/shard_map/reshape | solution.py:22
  84.7 4.6 %all-to-all-start = ((f32[32,6,1,512]{3,2,1,0:T(1,128)}), f32[32,6,1,512]{3,2,1,0:T(1,128)S(1)}, u32[]{:S(2)}, u32[]{:S(2)}) async-start(f32[32,6,1,512]{3,2,1,0:T(1,128)} %copy.54), calls=%async_computation.1 | async-start | bytes 786432 | tf_op jit(solution)/shard_map/all_to_all | solution.py:25
  89.3 0.8 copy.85
  90.1 11.7 %all-to-all-done = f32[32,6,1,512]{3,2,1,0:T(1,128)S(1)} async-done(((f32[32,6,1,512]{3,2,1,0:T(1,128)}), f32[32,6,1,512]{3,2,1,0:T(1,128)S(1)}, u32[]{:S(2)}, u32[]{:S(2)}) %all-to-all-start) | async-done | bytes 393248 | tf_op jit(solution)/shard_map/all_to_all | solution.py:25
  101.8 3.5 %all-to-all-start.3 = ((f32[4,6,8,1,512]{4,0,1,3,2:T(4,128)}), f32[4,6,8,1,512]{4,0,1,3,2:T(4,128)S(1)}, u32[]{:S(2)}, u32[]{:S(2)}) async-start(f32[4,6,8,1,512]{4,0,1,3,2:T(4,128)} %bitcast.51), calls=%async_computation.5 | async-start | bytes 786432 | tf_op jit(solution)/shard_map/all_to_all | solution.py:33
  105.4 0.8 copy.86
  106.3 5.2 %all-to-all-done.3 = f32[4,6,8,1,512]{4,0,1,3,2:T(4,128)S(1)} async-done(((f32[4,6,8,1,512]{4,0,1,3,2:T(4,128)}), f32[4,6,8,1,512]{4,0,1,3,2:T(4,128)S(1)}, u32[]{:S(2)}, u32[]{:S(2)}) %all-to-all-start.3) | async-done | bytes 393248 | tf_op jit(solution)/shard_map/all_to_all | solution.py:33
  111.5 3.5 %all-to-all-start.1 = ((f32[4,6,8,1,512]{4,0,1,3,2:T(4,128)}), f32[4,6,8,1,512]{4,0,1,3,2:T(4,128)S(1)}, u32[]{:S(2)}, u32[]{:S(2)}) async-start(f32[4,6,8,1,512]{4,0,1,3,2:T(4,128)} %bitcast.52), calls=%async_computation.2 | async-start | bytes 786432 | tf_op jit(solution)/shard_map/all_to_all | solution.py:32
  115.1 0.3 copy.77
  115.4 0.3 reshape.92
  115.7 5.1 %all-to-all-done.1 = f32[4,6,8,1,512]{4,0,1,3,2:T(4,128)S(1)} async-done(((f32[4,6,8,1,512]{4,0,1,3,2:T(4,128)}), f32[4,6,8,1,512]{4,0,1,3,2:T(4,128)S(1)}, u32[]{:S(2)}, u32[]{:S(2)}) %all-to-all-start.1) | async-done | bytes 393248 | tf_op jit(solution)/shard_map/all_to_all | solution.py:32
  120.9 0.3 copy.75
  121.1 0.3 reshape.91
  121.5 1.0 copy.71
  122.5 0.7 fusion.13
  123.2 0.8 multiply_reduce_fusion.2
  124.0 0.6 fusion.11
  124.6 1.2 fusion.20
  125.7 15.3 %all-reduce.1 = (f32[4,8,6]{2,1,0:T(8,128)S(1)}, f32[4,8]{1,0:T(4,128)S(1)}) all-reduce(f32[4,8,6]{2,1,0:T(8,128)S(1)} %fusion.20, f32[4,8]{1,0:T(4,128)S(1)} %get-tuple-element.26), channel_id=1, replica_groups=mesh['epoch'=4,'blend'=8] {'epoch'}, use_global_device_ids=true, to_apply=%region_5.0 | all-reduce | flops 224 | bytes 1792 | tf_op jit(solution)/shard_map/psum | solution.py:60
  141.3 0.7 fusion.3
  142.1 0.8 multiply_reduce_fusion.1
  142.8 0.7 fusion.1
  143.5 1.2 fusion.21
  144.7 15.1 %all-reduce = (f32[4,8,6]{2,1,0:T(8,128)S(1)}, f32[4,8]{1,0:T(4,128)S(1)}) all-reduce(f32[4,8,6]{2,1,0:T(8,128)S(1)} %fusion.21, f32[4,8]{1,0:T(4,128)S(1)} %get-tuple-element.28), channel_id=1, replica_groups=mesh['epoch'=4,'blend'=8] {'epoch'}, use_global_device_ids=true, to_apply=%region_9.0 | all-reduce | flops 224 | bytes 1792 | tf_op jit(solution)/shard_map/psum | solution.py:60
  159.9 0.7 copy.72
  (27 shorter events, 1.0 us)
Async XLA Ops:
  7.2 41.2 %reduce-scatter.5.cloned.1.call-start = ((), (), s32[]{:S(2)}) async-start(), calls=%async_computation.7 | async-start | bytes 1966080 | tf_op jit(solution)/shard_map/reduce_scatter | solution.py:19
  14.3 68.2 %reduce-scatter.3.cloned.1.call-start = ((), (), s32[]{:S(2)}) async-start(), calls=%async_computation.6 | async-start | bytes 1966080 | tf_op jit(solution)/shard_map/reduce_scatter | solution.py:18
  14.4 90.9 %copy-start.4 = (s32[4]{0:T(128)S(1)}, s32[4]{0:T(128)}, u32[]{:S(2)}) copy-start(s32[4]{0:T(128)} %param.11) | copy-start | bytes 52
  14.4 90.9 %copy-start.3 = (f32[4,8,6]{1,0,2:T(4,128)S(1)}, f32[4,8,6]{1,0,2:T(4,128)}, u32[]{:S(2)}) copy-start(f32[4,8,6]{1,0,2:T(4,128)} %param.12) | copy-start | bytes 2308
  50.5 34.1 %all-to-all-start.2 = ((f32[32,6,1,512]{3,2,1,0:T(1,128)}), f32[32,6,1,512]{3,2,1,0:T(1,128)S(1)}, u32[]{:S(2)}, u32[]{:S(2)}) async-start(f32[32,6,1,512]{3,2,1,0:T(1,128)} %copy.58), calls=%async_computation.4 | async-start | bytes 786432 | tf_op jit(solution)/shard_map/all_to_all | solution.py:26
  84.7 17.1 %all-to-all-start = ((f32[32,6,1,512]{3,2,1,0:T(1,128)}), f32[32,6,1,512]{3,2,1,0:T(1,128)S(1)}, u32[]{:S(2)}, u32[]{:S(2)}) async-start(f32[32,6,1,512]{3,2,1,0:T(1,128)} %copy.54), calls=%async_computation.1 | async-start | bytes 786432 | tf_op jit(solution)/shard_map/all_to_all | solution.py:25
  101.8 9.7 %all-to-all-start.3 = ((f32[4,6,8,1,512]{4,0,1,3,2:T(4,128)}), f32[4,6,8,1,512]{4,0,1,3,2:T(4,128)S(1)}, u32[]{:S(2)}, u32[]{:S(2)}) async-start(f32[4,6,8,1,512]{4,0,1,3,2:T(4,128)} %bitcast.51), calls=%async_computation.5 | async-start | bytes 786432 | tf_op jit(solution)/shard_map/all_to_all | solution.py:33
  111.5 9.3 %all-to-all-start.1 = ((f32[4,6,8,1,512]{4,0,1,3,2:T(4,128)}), f32[4,6,8,1,512]{4,0,1,3,2:T(4,128)S(1)}, u32[]{:S(2)}, u32[]{:S(2)}) async-start(f32[4,6,8,1,512]{4,0,1,3,2:T(4,128)} %bitcast.52), calls=%async_computation.2 | async-start | bytes 786432 | tf_op jit(solution)/shard_map/all_to_all | solution.py:32
  115.4 7.1 %copy-start = (s32[4,8,4096]{2,1,0:T(8,128)S(1)}, s32[4,8,4096]{2,1,0:T(8,128)}, u32[]{:S(2)}) copy-start(s32[4,8,4096]{2,1,0:T(8,128)} %param.10) | copy-start | bytes 1572868
  115.4 7.1 %copy-start.2 = (f32[4,8,4096]{2,1,0:T(8,128)S(1)}, f32[4,8,4096]{2,1,0:T(8,128)}, u32[]{:S(2)}) copy-start(f32[4,8,4096]{2,1,0:T(8,128)} %param.13) | copy-start | bytes 1572868
  142.8 17.7 %copy-start.1 = (f32[4,8,4096]{2,1,0:T(8,128)}, f32[4,8,4096]{2,1,0:T(8,128)S(1)}, u32[]{:S(2)}) copy-start(f32[4,8,4096]{2,1,0:T(8,128)S(1)} %get-tuple-element.29) | copy-start | bytes 1572868
Sparse Core Ops, SparseCore 0:
  14.5 33.8 reduce-scatter.4
  51.4 31.1 reduce-scatter.2
where the time goes:
time: 168 us; the launch traced here: 167 us
  waiting for transfers between devices  83.4 us (50%)
  blocking collectives  30.4 us (18%)
  starting transfers between devices  16.2 us (10%)
  between operations  14.2 us (8%)
  local copies, waits for them, and re-layouts  8.92 us (5%)
  other arithmetic  7.82 us (5%)
  matrix products  6.48 us (4%)
    reduce_scatter x1, waiting for transfers between devices, on_device(): lax.psum_scatter(weight_sum, 'epoch', scatter_dimension=2, tiled=True)  33.3 us
    psum x2, blocking collectives, on_device(): spectra_grad, morph_norm = lax.psum((spectra_grad, morph_norm), 'epoch')  30.4 us
    reduce_scatter x1, waiting for transfers between devices, on_device(): lax.psum_scatter(numerator, 'epoch', scatter_dimension=2, tiled=True)  27.4 us
    all_to_all x1, waiting for transfers between devices, on_device(): lax.all_to_all(numerator, 'blend', split_axis=0, concat_axis=2, tiled=True)  11.7 us
    reduce_sum x1, other arithmetic, on_device(): weight_sum = jnp.sum(weights, axis=0)  6.42 us
    all_to_all x1, waiting for transfers between devices, on_device(): lax.all_to_all(weight_sum, 'epoch', split_axis=2, concat_axis=3, tiled=True)  5.22 us
    all_to_all x1, waiting for transfers between devices, on_device(): lax.all_to_all(numerator, 'epoch', split_axis=2, concat_axis=3, tiled=True)  5.14 us
    all_to_all x1, starting transfers between devices, on_device(): lax.all_to_all(weight_sum, 'blend', split_axis=0, concat_axis=2, tiled=True)  4.59 us
  transfers between devices with their start and end apart: 6, of which 5 were waited for; matrix products, arithmetic and copies ran while one was open for 4% of the time, Pallas kernels for 0%

commit v1 on v0

--- a/solution.py
+++ b/solution.py
@@ -30,7 +30,12 @@
     weight_sum = weight_sum.reshape(owned, band_count, blocks, 1, piece)
     numerator, weight_sum = (
         lax.all_to_all(numerator, "epoch", split_axis=2, concat_axis=3, tiled=True),
-        lax.all_to_all(weight_sum, "epoch", split_axis=2, concat_axis=3, tiled=True),
+        jnp.concatenate(
+            lax.all_to_all(
+                jnp.stack(jnp.split(weight_sum, lax.axis_size("epoch"), axis=2)), "epoch", 0, 0
+            ),
+            axis=3,
+        ),
     )
     numerator = numerator.reshape(owned, band_count, pix_part)
     weight_sum = weight_sum.reshape(owned, band_count, pix_part)

time: 168 us -> 168 us (level)
  no operation moved by 1% of the time
where the time goes in v1:
time: 168 us; the launch traced here: 167 us
  waiting for transfers between devices  82.8 us (49%)
  blocking collectives  30.4 us (18%)
  starting transfers between devices  16.2 us (10%)
  between operations  14.2 us (8%)
  other arithmetic  8.74 us (5%)
  local copies, waits for them, and re-layouts  8.64 us (5%)
  matrix products  6.48 us (4%)
    reduce_scatter x1, waiting for transfers between devices, on_device(): lax.psum_scatter(weight_sum, 'epoch', scatter_dimension=2, tiled=True)  33.3 us
    psum x2, blocking collectives, on_device(): spectra_grad, morph_norm = lax.psum((spectra_grad, morph_norm), 'epoch')  30.4 us
    reduce_scatter x1, waiting for transfers between devices, on_device(): lax.psum_scatter(numerator, 'epoch', scatter_dimension=2, tiled=True)  27.4 us
    all_to_all x1, waiting for transfers between devices, on_device(): lax.all_to_all(numerator, 'blend', split_axis=0, concat_axis=2, tiled=True)  11 us
    reduce_sum x1, other arithmetic, on_device(): weight_sum = jnp.sum(weights, axis=0)  6.42 us
    all_to_all x1, waiting for transfers between devices, on_device(): lax.all_to_all(jnp.stack(jnp.split(weight_sum, lax.axis_size('epoch'), ax...  5.22 us
    all_to_all x1, waiting for transfers between devices, on_device(): lax.all_to_all(numerator, 'epoch', split_axis=2, concat_axis=3, tiled=True)  5.18 us
    all_to_all x1, starting transfers between devices, on_device(): lax.all_to_all(weight_sum, 'blend', split_axis=0, concat_axis=2, tiled=True)  4.59 us
  transfers between devices with their start and end apart: 6, of which 5 were waited for; matrix products, arithmetic and copies ran while one was open for 4% of the time, Pallas kernels for 0%

profile of v1, /device:TPU:0, one launch (start us, length us, event | category | flops | bytes accessed | tf_op | source)
XLA Modules:
  0.0 167.5 jit_solution(4045377614913481731)
XLA Ops:
  7.2 0.7 convert_element_type.23
  7.9 6.4 %fusion = (f32[32,6,2048]{2,0,1:T(8,128)}, f32[32,6,2048]{2,0,1:T(8,128)}) fusion(bf16[4,32,6,2048]{3,1,2,0:T(8,128)(2,1)} %param.8, f32[4,32]{1,0:T(4,128)S(1)} %convert_element_type.23, bf16[4,32,6,2048]{3,1,2,0:T(8,128)(2,1)} %param.7), kind=kLoop, calls=%fused_computation.2 | loop fusion | flops 8650752 | bytes 9437696 | tf_op jit(solution)/shard_map/reduce_sum | solution.py:14
  14.4 0.7 reduce-scatter.3.cloned.1.call-update
  15.1 33.3 %reduce-scatter.5.cloned.1.call-done = f32[32,6,512]{2,0,1:T(8,128)} async-done(((f32[32,6,2048]{2,0,1:T(8,128)}), f32[32,6,512]{2,0,1:T(8,128)}) %reduce-scatter.5.cloned.1.call-update) | async-done | bytes 393232 | tf_op jit(solution)/shard_map/reduce_scatter | solution.py:19
  48.4 2.2 %copy.129 = f32[32,6,1,512]{3,2,1,0:T(1,128)} copy(f32[32,6,1,512]{3,0,2,1:T(8,128)} %bitcast.62) | data formatting | bytes 786432 | tf_op jit(solution)/shard_map/reshape | solution.py:23
  50.5 4.6 %all-to-all-start.2 = ((f32[32,6,1,512]{3,2,1,0:T(1,128)}), f32[32,6,1,512]{3,2,1,0:T(1,128)S(1)}, u32[]{:S(2)}, u32[]{:S(2)}) async-start(f32[32,6,1,512]{3,2,1,0:T(1,128)} %copy.129), calls=%async_computation.4 | async-start | bytes 786432 | tf_op jit(solution)/shard_map/all_to_all | solution.py:26
  55.1 27.4 %reduce-scatter.3.cloned.1.call-done = f32[32,6,512]{2,0,1:T(8,128)} async-done(((f32[32,6,2048]{2,0,1:T(8,128)}), f32[32,6,512]{2,0,1:T(8,128)}) %reduce-scatter.3.cloned.1.call-update) | async-done | bytes 393232 | tf_op jit(solution)/shard_map/reduce_scatter | solution.py:18
  82.5 2.1 %copy.125 = f32[32,6,1,512]{3,2,1,0:T(1,128)} copy(f32[32,6,1,512]{3,0,1,2:T(8,128)} %bitcast.63) | data formatting | bytes 786432 | tf_op jit(solution)/shard_map/reshape | solution.py:22
  84.7 4.6 %all-to-all-start = ((f32[32,6,1,512]{3,2,1,0:T(1,128)}), f32[32,6,1,512]{3,2,1,0:T(1,128)S(1)}, u32[]{:S(2)}, u32[]{:S(2)}) async-start(f32[32,6,1,512]{3,2,1,0:T(1,128)} %copy.125), calls=%async_computation.1 | async-start | bytes 786432 | tf_op jit(solution)/shard_map/all_to_all | solution.py:25
  89.3 0.3 fusion.20
  89.9 0.9 pad_maximum_fusion
  90.8 11.0 %all-to-all-done = f32[32,6,1,512]{3,2,1,0:T(1,128)S(1)} async-done(((f32[32,6,1,512]{3,2,1,0:T(1,128)}), f32[32,6,1,512]{3,2,1,0:T(1,128)S(1)}, u32[]{:S(2)}, u32[]{:S(2)}) %all-to-all-start) | async-done | bytes 393248 | tf_op jit(solution)/shard_map/all_to_all | solution.py:25
  101.8 3.5 %all-to-all-start.3 = ((f32[4,4,6,2,1,512]{5,3,2,1,4,0:T(2,128)}), f32[4,4,6,2,1,512]{5,3,2,1,4,0:T(2,128)S(1)}, u32[]{:S(2)}, u32[]{:S(2)}) async-start(f32[4,4,6,2,1,512]{5,3,2,1,4,0:T(2,128)} %pad_maximum_fusion), calls=%async_computation.5 | async-start | bytes 786432 | tf_op jit(solution)/shard_map/all_to_all | solution.py:34
  105.4 0.8 copy.161
  106.3 5.2 %all-to-all-done.3 = f32[4,4,6,2,1,512]{5,3,2,1,4,0:T(2,128)S(1)} async-done(((f32[4,4,6,2,1,512]{5,3,2,1,4,0:T(2,128)}), f32[4,4,6,2,1,512]{5,3,2,1,4,0:T(2,128)S(1)}, u32[]{:S(2)}, u32[]{:S(2)}) %all-to-all-start.3) | async-done | bytes 393248 | tf_op jit(solution)/shard_map/all_to_all | solution.py:34
  111.5 3.5 %all-to-all-start.1 = ((f32[4,6,8,1,512]{4,0,1,3,2:T(4,128)}), f32[4,6,8,1,512]{4,0,1,3,2:T(4,128)S(1)}, u32[]{:S(2)}, u32[]{:S(2)}) async-start(f32[4,6,8,1,512]{4,0,1,3,2:T(4,128)} %bitcast.57), calls=%async_computation.2 | async-start | bytes 786432 | tf_op jit(solution)/shard_map/all_to_all | solution.py:32
  115.4 0.3 reshape.91
  115.6 5.2 %all-to-all-done.1 = f32[4,6,8,1,512]{4,0,1,3,2:T(4,128)S(1)} async-done(((f32[4,6,8,1,512]{4,0,1,3,2:T(4,128)}), f32[4,6,8,1,512]{4,0,1,3,2:T(4,128)S(1)}, u32[]{:S(2)}, u32[]{:S(2)}) %all-to-all-start.1) | async-done | bytes 393248 | tf_op jit(solution)/shard_map/all_to_all | solution.py:32
  120.9 0.3 copy.148
  121.1 0.3 reshape.90
  121.5 1.0 copy.144
  122.5 0.7 fusion.13
  123.2 0.8 multiply_reduce_fusion.2
  124.0 0.6 fusion.11
  124.6 1.2 fusion.21
  125.7 15.4 %all-reduce.1 = (f32[4,8,6]{2,1,0:T(8,128)S(1)}, f32[4,8]{1,0:T(4,128)S(1)}) all-reduce(f32[4,8,6]{2,1,0:T(8,128)S(1)} %fusion.21, f32[4,8]{1,0:T(4,128)S(1)} %get-tuple-element.39), channel_id=1, replica_groups=mesh['epoch'=4,'blend'=8] {'epoch'}, use_global_device_ids=true, to_apply=%region_5.0 | all-reduce | flops 224 | bytes 1792 | tf_op jit(solution)/shard_map/psum | solution.py:65
  141.4 0.7 fusion.3
  142.1 0.8 multiply_reduce_fusion.1
  142.9 0.7 fusion.1
  143.6 1.2 fusion.22
  144.7 15.1 %all-reduce = (f32[4,8,6]{2,1,0:T(8,128)S(1)}, f32[4,8]{1,0:T(4,128)S(1)}) all-reduce(f32[4,8,6]{2,1,0:T(8,128)S(1)} %fusion.22, f32[4,8]{1,0:T(4,128)S(1)} %get-tuple-element.41), channel_id=1, replica_groups=mesh['epoch'=4,'blend'=8] {'epoch'}, use_global_device_ids=true, to_apply=%region_9.0 | all-reduce | flops 224 | bytes 1792 | tf_op jit(solution)/shard_map/psum | solution.py:65
  159.9 0.7 copy.145
  (29 shorter events, 1.5 us)
Async XLA Ops:
  7.2 41.2 %reduce-scatter.5.cloned.1.call-start = ((), (), s32[]{:S(2)}) async-start(), calls=%async_computation.7 | async-start | bytes 1966080 | tf_op jit(solution)/shard_map/reduce_scatter | solution.py:19
  14.3 68.2 %reduce-scatter.3.cloned.1.call-start = ((), (), s32[]{:S(2)}) async-start(), calls=%async_computation.6 | async-start | bytes 1966080 | tf_op jit(solution)/shard_map/reduce_scatter | solution.py:18
  48.4 56.9 %copy-start.4 = (s32[4]{0:T(128)S(1)}, s32[4]{0:T(128)}, u32[]{:S(2)}) copy-start(s32[4]{0:T(128)} %param.11) | copy-start | bytes 52
  48.4 56.9 %copy-start.3 = (f32[4,8,6]{1,0,2:T(4,128)S(1)}, f32[4,8,6]{1,0,2:T(4,128)}, u32[]{:S(2)}) copy-start(f32[4,8,6]{1,0,2:T(4,128)} %param.12) | copy-start | bytes 2308
  50.5 34.1 %all-to-all-start.2 = ((f32[32,6,1,512]{3,2,1,0:T(1,128)}), f32[32,6,1,512]{3,2,1,0:T(1,128)S(1)}, u32[]{:S(2)}, u32[]{:S(2)}) async-start(f32[32,6,1,512]{3,2,1,0:T(1,128)} %copy.129), calls=%async_computation.4 | async-start | bytes 786432 | tf_op jit(solution)/shard_map/all_to_all | solution.py:26
  84.7 17.1 %all-to-all-start = ((f32[32,6,1,512]{3,2,1,0:T(1,128)}), f32[32,6,1,512]{3,2,1,0:T(1,128)S(1)}, u32[]{:S(2)}, u32[]{:S(2)}) async-start(f32[32,6,1,512]{3,2,1,0:T(1,128)} %copy.125), calls=%async_computation.1 | async-start | bytes 786432 | tf_op jit(solution)/shard_map/all_to_all | solution.py:25
  101.8 9.7 %all-to-all-start.3 = ((f32[4,4,6,2,1,512]{5,3,2,1,4,0:T(2,128)}), f32[4,4,6,2,1,512]{5,3,2,1,4,0:T(2,128)S(1)}, u32[]{:S(2)}, u32[]{:S(2)}) async-start(f32[4,4,6,2,1,512]{5,3,2,1,4,0:T(2,128)} %pad_maximum_fusion), calls=%async_computation.5 | async-start | bytes 786432 | tf_op jit(solution)/shard_map/all_to_all | solution.py:34
  111.5 9.3 %all-to-all-start.1 = ((f32[4,6,8,1,512]{4,0,1,3,2:T(4,128)}), f32[4,6,8,1,512]{4,0,1,3,2:T(4,128)S(1)}, u32[]{:S(2)}, u32[]{:S(2)}) async-start(f32[4,6,8,1,512]{4,0,1,3,2:T(4,128)} %bitcast.57), calls=%async_computation.2 | async-start | bytes 786432 | tf_op jit(solution)/shard_map/all_to_all | solution.py:32
  115.3 7.2 %copy-start = (s32[4,8,4096]{2,1,0:T(8,128)S(1)}, s32[4,8,4096]{2,1,0:T(8,128)}, u32[]{:S(2)}) copy-start(s32[4,8,4096]{2,1,0:T(8,128)} %param.10) | copy-start | bytes 1572868
  115.4 7.1 %copy-start.2 = (f32[4,8,4096]{2,1,0:T(8,128)S(1)}, f32[4,8,4096]{2,1,0:T(8,128)}, u32[]{:S(2)}) copy-start(f32[4,8,4096]{2,1,0:T(8,128)} %param.13) | copy-start | bytes 1572868
  142.9 17.8 %copy-start.1 = (f32[4,8,4096]{2,1,0:T(8,128)}, f32[4,8,4096]{2,1,0:T(8,128)S(1)}, u32[]{:S(2)}) copy-start(f32[4,8,4096]{2,1,0:T(8,128)S(1)} %get-tuple-element.42) | copy-start | bytes 1572868
Sparse Core Ops, SparseCore 0:
  14.5 33.8 reduce-scatter.4
  51.4 31.1 reduce-scatter.2
